TPU v7x, 16 devices: a 4x2x1 block of a 4x4x8 slice. The times are simulated.
16 devices in a mesh: dp: 4 (over y, z, core), sp: 4 (over x).
Axes of the slice: x: 4, y: 2, z: 1, core: 2. Of those that a mesh axis runs over, the one named last changes fastest.
The devices are a block of a 4x4x8 slice.
Arguments:
- q: bfloat16 [128, 8, 256], P('dp'), parts along dimension 0
- k: bfloat16 [128, 2048, 8, 256], P('dp', 'sp'), parts along dimension 0
- v: bfloat16 [128, 2048, 8, 256], P('dp', 'sp'), parts along dimension 0
Outputs:
- q: bfloat16 [128, 8, 256], P('dp'), parts along dimension 0
There are 4 independent parts. A program takes and returns all parts, laid end to end along the dimension named above; each array names one.
All inputs are finite; a program needn't handle non-finite values.
Results may differ from a plain program's by a relative error of at most 0.012.
Values are sent between devices in bfloat16 or wider.
A program may use at most 768 MiB of HBM per device.

v0:
```python
import jax
import jax.numpy as jnp
from jax import lax
from jax.sharding import PartitionSpec as P


def einsum(form, a, b):
    return jnp.einsum(form, a.astype(jnp.float32), b.astype(jnp.float32))


def part_of(q, k, v):
    grouped = q.reshape(q.shape[0], k.shape[2], -1, q.shape[2])
    scores = einsum("bgsd,bugd->bgsu", grouped, k) * q.shape[2] ** -0.5
    high = jnp.max(scores, -1, keepdims=True)
    weights = jnp.exp(scores - high)
    seen = einsum("bgsu,bugd->bgsd", weights.astype(jnp.bfloat16), v)
    return jnp.concatenate([seen, jnp.sum(weights, -1, keepdims=True), high], -1)


def together(parts):
    seen, total, high = parts[..., :-2], parts[..., -2:-1], parts[..., -1:]
    scale = jnp.exp(high - jnp.max(high, 0))
    return (jnp.sum(seen * scale, 0) / jnp.sum(total * scale, 0)).astype(jnp.bfloat16)


def solution(mesh):
    def step(q, k, v):
        return together(lax.all_gather(part_of(q, k, v), "sp")).reshape(q.shape)

    return jax.shard_map(
        step,
        mesh=mesh,
        in_specs=(P("dp", None, None), P("dp", "sp", None, None), P("dp", "sp", None, None)),
        out_specs=P("dp", None, None),
        check_vma=False,
    )
```

profile of v0, /device:TPU:112, one launch (start us, length us, event | category | flops | bytes accessed | tf_op | source)
XLA Modules:
  0.0 110.7 jit_solution(9661360894254154000)
XLA Ops:
  6.5 0.0 all-gather.3.cloned.1.call-start
  6.6 31.9 %fusion.2 = f32[32,8,1,512]{3,2,1,0:T(1,128)S(1)} fusion(bf16[32,512,8,256]{3,2,1,0:T(8,128)(2,1)} %param.4, bf16[32,8,256,1]{2,1,0,3:T(8,128)(2,1)} %bitcast.26), kind=kOutput, calls=%fused_computation.2 | convolution fusion | flops 67108864 | bytes 67764224 | tf_op jit(solution)/shard_map/bgsd,bugd->bgsu/dot_general | solution.py:8
  38.4 0.1 fusion.9
  38.5 0.2 fusion.10
  38.8 32.5 %fusion = f32[32,8,1,256]{3,2,1,0:T(1,128)S(1)} fusion(bf16[32,512,8,256]{3,2,1,0:T(8,128)(2,1)} %param.5, bf16[32,8,512,1]{2,1,0,3:T(8,128)(2,1)S(1)} %get-tuple-element.7), kind=kOutput, calls=%fused_computation | convolution fusion | flops 67108864 | bytes 67633152 | tf_op jit(solution)/shard_map/bgsu,bugd->bgsd/dot_general | solution.py:8
  71.3 0.3 copy.23
  71.5 0.3 copy.22
  71.8 0.8 pad_maximum_fusion
  72.6 0.1 all-gather.3.cloned.1.call-update
  72.7 25.2 %all-gather.3.cloned.1.call-done = f32[128,8,1,258]{3,1,2,0:T(8,128)} async-done(((f32[32,8,1,258]{3,1,2,0:T(8,128)}), f32[128,8,1,258]{3,1,2,0:T(8,128)}) %all-gather.3.cloned.1.call-update) | async-done | bytes 1056784 | tf_op jit(solution)/shard_map/all_gather | solution.py:28
  97.9 1.3 %slice_reduce_fusion = f32[32,8]{1,0:T(8,128)S(1)} fusion(f32[4,32,8,1,258]{4,2,1,0,3:T(8,128)} %bitcast.22), kind=kLoop, calls=%fused_computation.12 | loop fusion | flops 768 | bytes 5120 | tf_op jit(solution)/shard_map/reduce_max | solution.py:22
  99.2 1.6 %fusion.5 = (f32[32,8]{1,0:T(8,128)S(1)}, f32[4,32,8,1,1]{4,2,1,0,3:T(8,128)S(1)}) fusion(f32[4,32,8,1,258]{4,2,1,0,3:T(8,128)} %bitcast.23, f32[32,8]{1,0:T(8,128)S(1)} %slice_reduce_fusion), kind=kLoop, calls=%fused_computation.7 | loop fusion | flops 2816 | bytes 14336 | tf_op jit(solution)/shard_map/reduce_sum | solution.py:23
  100.8 0.8 copy.36
  101.7 1.5 %fusion.4 = f32[32,8,256]{2,1,0:T(8,128)S(1)} fusion(f32[4,32,8,1,258]{4,2,1,0,3:T(8,128)} %bitcast.24, f32[4,32,8]{2,1,0:T(8,128)S(1)} %bitcast.27), kind=kLoop, calls=%fused_computation.5 | loop fusion | flops 458752 | bytes 1314816 | tf_op jit(solution)/shard_map/reduce_sum | solution.py:23
  103.1 0.8 divide_convert_fusion
  (1 shorter events, 0.0 us)
Async XLA Ops:
  6.5 91.4 %all-gather.3.cloned.1.call-start = ((), (), s32[]{:S(2)}) async-start(), calls=%async_computation | async-start | bytes 1966080 | tf_op jit(solution)/shard_map/all_gather | solution.py:28
Sparse Core Ops, SparseCore 0:
  72.8 25.0 all-gather.2
where the time goes:
time: 111 us
  matrix products  64.3 us (58%)
  waiting for transfers between devices  25.3 us (23%)
  between operations  13.5 us (12%)
  other arithmetic  6.36 us (6%)
  local copies, waits for them, and re-layouts  1.35 us (1%)
    dot_general x2, matrix products, einsum(): return jnp.einsum(form, a.astype(jnp.float32), b.astype(jnp.float32))  64.3 us
    all_gather x1, waiting for transfers between devices, step(): return together(lax.all_gather(part_of(q, k, v), 'sp')).reshape(q.shape)  25.2 us
  transfers between devices with their start and end apart: 1, of which 1 were waited for; matrix products, arithmetic and copies ran while one was open for 0% of the time, Pallas kernels for 0%

commit v1 on v0

v1 whole, which is shorter than its diff:
```python
import functools

import jax
import jax.numpy as jnp
from jax import lax
from jax.experimental import pallas as pl
from jax.experimental.pallas import tpu as pltpu
from jax.sharding import PartitionSpec as P

SLOTS = 6


def kernel(axis, runs, scale, q_ref, k_ref, v_ref, out_ref, k_buf, v_buf, parts, k_sem, v_sem, send_sem, recv_sem):
    count, rows, head = k_ref.shape
    heads = q_ref.shape[1]
    me = lax.axis_index(axis)

    def fetch(b):
        slot = lax.rem(b, SLOTS)
        pltpu.make_async_copy(k_ref.at[b], k_buf.at[slot], k_sem.at[slot]).start()
        pltpu.make_async_copy(v_ref.at[b], v_buf.at[slot], v_sem.at[slot]).start()

    for b in range(SLOTS):
        fetch(b)

    barrier = pltpu.get_barrier_semaphore()
    for ahead in range(1, runs):
        pl.semaphore_signal(barrier, inc=1, device_id={axis: lax.rem(me + ahead, runs)})
    pl.semaphore_wait(barrier, runs - 1)

    own = lax.broadcasted_iota(jnp.int32, (heads, rows), 1) % heads == lax.broadcasted_iota(jnp.int32, (heads, rows), 0)

    def send(b, ahead):
        return pltpu.make_async_remote_copy(
            src_ref=parts.at[0, b],
            dst_ref=parts.at[ahead, b],
            send_sem=send_sem.at[ahead - 1, b],
            recv_sem=recv_sem.at[ahead - 1, b],
            device_id={axis: lax.rem(me + ahead, runs)},
        )

    def attend(b, _):
        slot = lax.rem(b, SLOTS)
        pltpu.make_async_copy(k_ref.at[b], k_buf.at[slot], k_sem.at[slot]).wait()
        scores = lax.dot_general(q_ref[b], k_buf[slot], (((1,), (1,)), ((), ())), preferred_element_type=jnp.float32)
        scores = jnp.where(own, scores * scale, -jnp.inf)
        high = jnp.max(scores, -1, keepdims=True)
        weights = jnp.exp(scores - high)
        total = jnp.sum(weights, -1, keepdims=True)
        pltpu.make_async_copy(v_ref.at[b], v_buf.at[slot], v_sem.at[slot]).wait()
        seen = jnp.dot(weights.astype(jnp.bfloat16), v_buf[slot], preferred_element_type=jnp.float32)
        parts[0, b, :, :head] = seen
        lane = lax.broadcasted_iota(jnp.int32, (heads, 128), 1)
        parts[0, b, :, head:] = jnp.where(lane < 64, total, high)
        for ahead in range(1, runs):
            send(b, ahead).start()

        @pl.when(b + SLOTS < count)
        def _():
            fetch(b + SLOTS)

        return 0

    lax.fori_loop(0, count, attend, 0)

    def finish(b, _):
        for ahead in range(1, runs):
            send(b, ahead).wait()
        total = [parts[run, b, :, head : head + 1] for run in range(runs)]
        high = [parts[run, b, :, head + 64 : head + 65] for run in range(runs)]
        top = functools.reduce(jnp.maximum, high)
        rescale = [jnp.exp(h - top) for h in high]
        seen = sum(parts[run, b, :, :head] * rescale[run] for run in range(runs))
        out_ref[b] = (seen / sum(t * r for t, r in zip(total, rescale))).astype(out_ref.dtype)
        return 0

    lax.fori_loop(0, count, finish, 0)


def solution(mesh):
    axis = "sp"
    runs = mesh.shape[axis]

    def step(q, k, v):
        count, tokens, heads, head = k.shape
        rows = tokens * heads
        return pl.pallas_call(
            functools.partial(kernel, axis, runs, head**-0.5),
            out_shape=jax.ShapeDtypeStruct(q.shape, q.dtype),
            in_specs=[
                pl.BlockSpec(memory_space=pltpu.VMEM),
                pl.BlockSpec(memory_space=pl.ANY),
                pl.BlockSpec(memory_space=pl.ANY),
            ],
            out_specs=pl.BlockSpec(memory_space=pltpu.VMEM),
            scratch_shapes=[
                pltpu.VMEM((SLOTS, rows, head), k.dtype),
                pltpu.VMEM((SLOTS, rows, head), v.dtype),
                pltpu.VMEM((runs, count, heads, head + 128), jnp.float32),
                pltpu.SemaphoreType.DMA((SLOTS,)),
                pltpu.SemaphoreType.DMA((SLOTS,)),
                pltpu.SemaphoreType.DMA((runs - 1, count)),
                pltpu.SemaphoreType.DMA((runs - 1, count)),
            ],
            compiler_params=pltpu.CompilerParams(
                collective_id=0, has_side_effects=True, vmem_limit_bytes=56 << 20
            ),
            name="attend",
        )(q, k.reshape(count, rows, head), v.reshape(count, rows, head))

    return jax.shard_map(
        step,
        mesh=mesh,
        in_specs=(P("dp", None, None), P("dp", "sp", None, None), P("dp", "sp", None, None)),
        out_specs=P("dp", None, None),
        check_vma=False,
    )
```

time: 111 us -> 71.5 us (0.64)
  Pallas kernels: 0 us -> 69.8 us
  matrix products: 64.3 us -> 0 us
  waiting for transfers between devices: 25.3 us -> 0 us
  between operations: 13.5 us -> 0.01 us
  other arithmetic: 6.36 us -> 0 us
    pallas_call x0 -> x1, Pallas kernels: none -> 69.8 us  [step(): pl.pallas_call(functools.partial(kernel, axis, runs, head ** (-0.5)), out...]
    dot_general x2 -> x0, matrix products: 64.3 us -> none  [einsum(): return jnp.einsum(form, a.astype(jnp.float32), b.astype(jnp.float32))]
    all_gather x1 -> x0, waiting for transfers between devices: 25.2 us -> none  [step(): return together(lax.all_gather(part_of(q, k, v), 'sp')).reshape(q.shape)]
    reduce_sum x2 -> x0, other arithmetic: 3.08 us -> none  [the longest x1 1.61 us: together(): jnp.sum(total * scale, 0)]
    unnamed x0 -> x1, local copies, waits for them, and re-layouts: none -> 1.57 us
    reduce_max x2 -> x0, other arithmetic: 1.44 us -> none  [the longest x1 1.32 us: together(): scale = jnp.exp(high - jnp.max(high, 0))]
  transfers between devices with their start and end apart: 1 -> 0, of which waited for: 1 -> 0; matrix products, arithmetic and copies ran while one was open for 0% -> 0% of each run, Pallas kernels for 0% -> 0%
where the time goes in v1:
time: 71.5 us; the launch traced here: 71.4 us
  Pallas kernels  69.8 us (98%)
  local copies, waits for them, and re-layouts  1.57 us (2%)
    pallas_call x1, Pallas kernels, step(): pl.pallas_call(functools.partial(kernel, axis, runs, head ** (-0.5)), out...  69.8 us
    unnamed x1, local copies, waits for them, and re-layouts  1.57 us

profile of v1, /device:TPU:112, one launch (start us, length us, event | category | flops | bytes accessed | tf_op | source)
XLA Modules:
  0.0 71.4 jit_solution(13392637672236817482)
XLA Ops:
  0.0 69.8 %attend.1 = bf16[32,8,256]{2,1,0:T(8,128)(2,1)} custom-call(bf16[32,8,256]{2,1,0:T(8,128)(2,1)} %q_ref.1, bf16[32,4096,256]{2,1,0:T(8,128)(2,1)} %bitcast.k_ref, bf16[32,4096,256]{2,1,0:T(8,128)(2,1)} %bitcast.1.v_ref), custom_call_target="tpu_custom_call" | custom-call | tf_op jit(solution)/shard_map/attend/pallas_call | solution.py:87
  69.8 1.6 %copy.5 = bf16[32,8,256]{2,1,0:T(8,128)(2,1)} copy(bf16[32,8,256]{2,1,0:T(8,128)(2,1)} %attend.1) | data formatting | bytes 262144

commit v2 on v0

v2 whole, which is shorter than its diff:
```python
import functools

import jax
import jax.numpy as jnp
from jax import lax
from jax.experimental import pallas as pl
from jax.experimental.pallas import tpu as pltpu
from jax.sharding import PartitionSpec as P

PAIR = 2
SLOTS = 4
PIECES = 4
UNROLL = 5
LEAD = 2
LANES = 128


def kernel(axis, runs, scale, q_hbm, k_ref, v_ref, out_ref, q_ref, k_buf, v_buf, even, odd, seen, stats, q_sem, k_sem, v_sem, last_sem, send_sem, recv_sem):
    _, heads, head = q_ref.shape
    count, rows, _ = k_ref.shape
    steps = count // PAIR
    me = lax.axis_index(axis)

    def k_copy(i):
        slot = lax.rem(i, SLOTS)
        return pltpu.make_async_copy(k_ref.at[pl.ds(i * PAIR, PAIR)], k_buf.at[slot], k_sem.at[slot])

    def v_copy(i):
        slot = lax.rem(i, SLOTS)
        return pltpu.make_async_copy(v_ref.at[pl.ds(i * PAIR, PAIR)], v_buf.at[slot], v_sem.at[slot])

    pieces = ((0, 0, rows), (1, 0, rows // 2), (1, rows // 2, rows // 4), (1, 3 * rows // 4, rows // 4))
    last_slot = (steps - 1) % SLOTS

    def last_copy(piece):
        j, start, size = pieces[piece]
        part = pl.ds(start, size)
        return pltpu.make_async_copy(
            v_ref.at[count - PAIR + j, part], v_buf.at[last_slot, j, part], last_sem.at[piece]
        )

    q_copy = pltpu.make_async_copy(q_hbm, q_ref, q_sem)
    q_copy.start()
    for i in range(SLOTS):
        k_copy(i).start()
    for i in range(SLOTS):
        v_copy(i).start()

    barrier = pltpu.get_barrier_semaphore()
    for ahead in range(1, runs):
        pl.semaphore_signal(barrier, inc=1, device_id={axis: lax.rem(me + ahead, runs)})

    lane = lax.broadcasted_iota(jnp.int32, (heads, LANES), 1)
    own = lane % heads == lax.broadcasted_iota(jnp.int32, (heads, LANES), 0)
    quarter = lane // (LANES // 4)

    EARLY_SEEN, EARLY_STATS, LAST_SEEN, LAST_STATS = range(4)

    def to_peers(kind, index):
        ref = seen if kind in (EARLY_SEEN, LAST_SEEN) else stats
        for ahead in range(1, runs):
            yield pltpu.make_async_remote_copy(
                src_ref=ref.at[me, index],
                dst_ref=ref.at[me, index],
                send_sem=send_sem.at[kind % 2, ahead - 1],
                recv_sem=recv_sem.at[kind, ahead - 1],
                device_id={axis: lax.rem(me + ahead, runs)},
            )

    def send(kind, index):
        for copy in to_peers(kind, index):
            copy.start()

    def received(kind, index):
        for copy in to_peers(kind, index):
            copy.wait_recv()

    def score(i, scores, tops):
        slot = lax.rem(i, SLOTS)
        for j in range(PAIR):
            s = lax.dot_general(
                q_ref[i * PAIR + j], k_buf[slot, j], (((1,), (1,)), ((), ())), preferred_element_type=jnp.float32
            )
            s = [jnp.where(own, s[:, c : c + LANES] * scale, -jnp.inf) for c in range(0, rows, LANES)]
            high = jnp.max(functools.reduce(jnp.maximum, s), -1, keepdims=True)
            tops[j] = jnp.broadcast_to(high, (heads, LANES))
            scores[j] = jnp.concatenate(s, 1)

    def weigh(scores, tops, weights, totals):
        for j in range(PAIR):
            high = tops[j]
            total = None
            for c in range(0, rows, LANES):
                w = jnp.exp(scores[j, :, c : c + LANES] - high)
                total = w if total is None else total + w
                weights[j, :, c : c + LANES] = w.astype(weights.dtype)
            totals[j] = jnp.broadcast_to(jnp.sum(total, -1, keepdims=True), (heads, LANES))

    def mix(weights, slot, j, start, size):
        part = pl.ds(start, size)
        return jnp.dot(weights[j, :, part], v_buf[slot, j, part], preferred_element_type=jnp.float32)

    def gathered(totals, tops):
        return jnp.where(
            quarter == 0, totals[0], jnp.where(quarter == 1, tops[0], jnp.where(quarter == 2, totals[1], tops[1]))
        )

    def combine(i):
        stat = [stats[run, i] for run in range(runs)]
        wide = LANES // 4
        for j in range(PAIR):
            total = [s[:, 2 * wide * j : 2 * wide * j + 1] for s in stat]
            high = [s[:, 2 * wide * j + wide : 2 * wide * j + wide + 1] for s in stat]
            top = functools.reduce(jnp.maximum, high)
            rescale = [jnp.exp(h - top) for h in high]
            over = 1 / sum(t * r for t, r in zip(total, rescale))
            b = i * PAIR + j
            out_ref[b] = sum(seen[run, b].astype(jnp.float32) * (r * over) for run, r in enumerate(rescale)).astype(
                out_ref.dtype
            )

    q_copy.wait()

    for i in range(LEAD):
        k_copy(i).wait()
        score(i, *(even, odd)[i % 2][:2])
        k_copy(i + SLOTS).start()
    weigh(*even)
    pl.semaphore_wait(barrier, runs - 1)

    def advance(i, this, other, more):
        if more:
            k_copy(i + LEAD).wait()
        v_copy(i).wait()
        _, tops, weights, totals = this
        own_totals, own_tops = totals[...], tops[...]
        if more:
            score(i + LEAD, *this[:2])
        weigh(*other)
        for j in range(PAIR):
            seen[me, i * PAIR + j] = mix(weights, lax.rem(i, SLOTS), j, 0, rows).astype(seen.dtype)
        stats[me, i] = gathered(own_totals, own_tops)
        send(EARLY_SEEN, pl.ds(i * PAIR, PAIR))
        send(EARLY_STATS, i)

    def refill(i):
        @pl.when(i + LEAD + SLOTS < steps)
        def _():
            k_copy(i + LEAD + SLOTS).start()

        @pl.when(i + SLOTS < steps - 1)
        def _():
            v_copy(i + SLOTS).start()

        @pl.when(i + SLOTS == steps - 1)
        def _():
            for piece in range(PIECES):
                last_copy(piece).start()

    def body(m, _):
        advance(2 * m, even, odd, True)
        refill(2 * m)
        advance(2 * m + 1, odd, even, True)
        refill(2 * m + 1)
        return 0

    lax.fori_loop(0, (steps - LEAD) // 2, body, 0)
    advance(steps - 2, even, odd, False)
    _, tops, weights, totals = odd
    stats[me, steps - 1] = gathered(totals[...], tops[...])
    send(LAST_STATS, steps - 1)
    sums = None
    for piece, (j, start, size) in enumerate(pieces):
        last_copy(piece).wait()
        more = mix(weights, last_slot, j, start, size)
        sums = more if start == 0 else sums + more
        if start + size == rows:
            seen[me, count - PAIR + j] = sums.astype(seen.dtype)
            send(LAST_SEEN, count - PAIR + j)

    received(EARLY_SEEN, pl.ds(0, count - PAIR))
    received(EARLY_STATS, pl.ds(0, steps - 1))

    def finish(i, _):
        combine(i)
        return 0

    lax.fori_loop(0, steps - 1, finish, 0, unroll=UNROLL)
    received(LAST_STATS, steps - 1)
    received(LAST_SEEN, pl.ds(count - PAIR, PAIR))
    combine(steps - 1)
    for kind, index in ((EARLY_SEEN, pl.ds(0, count)), (EARLY_STATS, pl.ds(0, steps))):
        for copy in to_peers(kind, index):
            copy.wait_send()


def solution(mesh):
    axis = "sp"
    runs = mesh.shape[axis]

    def step(q, k, v):
        count, tokens, heads, head = k.shape
        rows = tokens * heads
        steps = count // PAIR
        step_buffers = (
            pltpu.VMEM((PAIR, heads, rows), jnp.float32),
            pltpu.VMEM((PAIR, heads, LANES), jnp.float32),
            pltpu.VMEM((PAIR, heads, rows), v.dtype),
            pltpu.VMEM((PAIR, heads, LANES), jnp.float32),
        )
        return pl.pallas_call(
            functools.partial(kernel, axis, runs, head**-0.5),
            out_shape=jax.ShapeDtypeStruct(q.shape, q.dtype),
            in_specs=[pl.BlockSpec(memory_space=pltpu.HBM)] * 3,
            out_specs=pl.BlockSpec(memory_space=pltpu.VMEM),
            scratch_shapes=[
                pltpu.VMEM(q.shape, q.dtype),
                pltpu.VMEM((SLOTS, PAIR, rows, head), k.dtype),
                pltpu.VMEM((SLOTS, PAIR, rows, head), v.dtype),
                step_buffers,
                step_buffers,
                pltpu.VMEM((runs, count, heads, head), q.dtype),
                pltpu.VMEM((runs, steps, heads, LANES), jnp.float32),
                pltpu.SemaphoreType.DMA,
                pltpu.SemaphoreType.DMA((SLOTS,)),
                pltpu.SemaphoreType.DMA((SLOTS,)),
                pltpu.SemaphoreType.DMA((PIECES,)),
                pltpu.SemaphoreType.DMA((2, runs - 1)),
                pltpu.SemaphoreType.DMA((4, runs - 1)),
            ],
            compiler_params=pltpu.CompilerParams(
                collective_id=0, has_side_effects=True, vmem_limit_bytes=40 << 20
            ),
            name="attend",
        )(pltpu.with_memory_space_constraint(q, pltpu.HBM), k.reshape(count, rows, head), v.reshape(count, rows, head))

    return jax.shard_map(
        step,
        mesh=mesh,
        in_specs=(P("dp", None, None), P("dp", "sp", None, None), P("dp", "sp", None, None)),
        out_specs=P("dp", None, None),
        check_vma=False,
    )
```

time: 111 us -> 48.3 us (0.44)
  matrix products: 64.3 us -> 0 us
  Pallas kernels: 0 us -> 47.6 us
  waiting for transfers between devices: 25.3 us -> 0 us
  between operations: 13.5 us -> 0.01 us
  other arithmetic: 6.36 us -> 0 us
    dot_general x2 -> x0, matrix products: 64.3 us -> none  [einsum(): return jnp.einsum(form, a.astype(jnp.float32), b.astype(jnp.float32))]
    pallas_call x0 -> x1, Pallas kernels: none -> 47.6 us  [step(): pl.pallas_call(functools.partial(kernel, axis, runs, head ** (-0.5)), out...]
    all_gather x1 -> x0, waiting for transfers between devices: 25.2 us -> none  [step(): return together(lax.all_gather(part_of(q, k, v), 'sp')).reshape(q.shape)]
    reduce_sum x2 -> x0, other arithmetic: 3.08 us -> none  [the longest x1 1.61 us: together(): jnp.sum(total * scale, 0)]
    reduce_max x2 -> x0, other arithmetic: 1.44 us -> none  [the longest x1 1.32 us: together(): scale = jnp.exp(high - jnp.max(high, 0))]
  transfers between devices with their start and end apart: 1 -> 0, of which waited for: 1 -> 0; matrix products, arithmetic and copies ran while one was open for 0% -> 0% of each run, Pallas kernels for 0% -> 0%
where the time goes in v2:
time: 48.3 us; the launch traced here: 48.2 us
  Pallas kernels  47.6 us (99%)
  local copies, waits for them, and re-layouts  0.66 us (1%)
    pallas_call x1, Pallas kernels, step(): pl.pallas_call(functools.partial(kernel, axis, runs, head ** (-0.5)), out...  47.6 us

profile of v2, /device:TPU:112, one launch (start us, length us, event | category | flops | bytes accessed | tf_op | source)
XLA Modules:
  0.0 48.2 jit_solution(9883687920028065306)
XLA Ops:
  0.0 47.6 %attend.1 = bf16[32,8,256]{2,1,0:T(8,128)(2,1)S(1)} custom-call(bf16[32,8,256]{2,1,0:T(8,128)(2,1)} %q_hbm.1, bf16[32,4096,256]{2,1,0:T(8,128)(2,1)} %bitcast.k_ref, bf16[32,4096,256]{2,1,0:T(8,128)(2,1)} %bitcast.1.v_ref), custom_call_target="tpu_custom_call" | custom-call | tf_op jit(solution)/shard_map/attend/pallas_call | solution.py:211
  47.6 0.7 %copy.5 = bf16[32,8,256]{2,1,0:T(8,128)(2,1)} copy(bf16[32,8,256]{2,1,0:T(8,128)(2,1)S(1)} %attend.1) | data formatting | bytes 262144

commit v3 on v2

--- a/solution.py
+++ b/solution.py
@@ -9,13 +9,13 @@
 
 PAIR = 2
 SLOTS = 4
-PIECES = 4
+PIECES = 2
 UNROLL = 5
-LEAD = 2
+LEAD = 3
 LANES = 128
 
 
-def kernel(axis, runs, scale, q_hbm, k_ref, v_ref, out_ref, q_ref, k_buf, v_buf, even, odd, seen, stats, q_sem, k_sem, v_sem, last_sem, send_sem, recv_sem):
+def kernel(axis, runs, scale, q_hbm, k_ref, v_ref, out_ref, q_ref, k_buf, v_buf, sets, seen, stats, q_sem, k_sem, v_sem, last_sem, send_sem, recv_sem):
     _, heads, head = q_ref.shape
     count, rows, _ = k_ref.shape
     steps = count // PAIR
@@ -29,21 +29,20 @@
         slot = lax.rem(i, SLOTS)
         return pltpu.make_async_copy(v_ref.at[pl.ds(i * PAIR, PAIR)], v_buf.at[slot], v_sem.at[slot])
 
-    pieces = ((0, 0, rows), (1, 0, rows // 2), (1, rows // 2, rows // 4), (1, 3 * rows // 4, rows // 4))
+    pieces = [(0, 3 * rows // 4), (3 * rows // 4, rows // 4)]
     last_slot = (steps - 1) % SLOTS
 
     def last_copy(piece):
-        j, start, size = pieces[piece]
-        part = pl.ds(start, size)
+        part = pl.ds(*pieces[piece])
         return pltpu.make_async_copy(
-            v_ref.at[count - PAIR + j, part], v_buf.at[last_slot, j, part], last_sem.at[piece]
+            v_ref.at[pl.ds(count - PAIR, PAIR), part], v_buf.at[last_slot, :, part], last_sem.at[piece]
         )
 
     q_copy = pltpu.make_async_copy(q_hbm, q_ref, q_sem)
     q_copy.start()
     for i in range(SLOTS):
         k_copy(i).start()
-    for i in range(SLOTS):
+    for i in range(SLOTS - LEAD):
         v_copy(i).start()
 
     barrier = pltpu.get_barrier_semaphore()
@@ -123,12 +122,14 @@
 
     for i in range(LEAD):
         k_copy(i).wait()
-        score(i, *(even, odd)[i % 2][:2])
+        score(i, *sets[i][:2])
         k_copy(i + SLOTS).start()
-    weigh(*even)
+        v_copy(i + SLOTS - LEAD).start()
+    weigh(*sets[0])
     pl.semaphore_wait(barrier, runs - 1)
 
-    def advance(i, this, other, more):
+    def advance(i, turn, more):
+        this, other = sets[turn], sets[(turn + 1) % LEAD]
         if more:
             k_copy(i + LEAD).wait()
         v_copy(i).wait()
@@ -158,25 +159,25 @@
                 last_copy(piece).start()
 
     def body(m, _):
-        advance(2 * m, even, odd, True)
-        refill(2 * m)
-        advance(2 * m + 1, odd, even, True)
-        refill(2 * m + 1)
+        for turn in range(LEAD):
+            advance(LEAD * m + turn, turn, True)
+            refill(LEAD * m + turn)
         return 0
 
-    lax.fori_loop(0, (steps - LEAD) // 2, body, 0)
-    advance(steps - 2, even, odd, False)
-    _, tops, weights, totals = odd
+    looped = (steps - LEAD) // LEAD
+    lax.fori_loop(0, looped, body, 0)
+    for i in range(LEAD * looped, steps - 1):
+        advance(i, i % LEAD, i + LEAD < steps)
+    _, tops, weights, totals = sets[(steps - 1) % LEAD]
     stats[me, steps - 1] = gathered(totals[...], tops[...])
     send(LAST_STATS, steps - 1)
-    sums = None
-    for piece, (j, start, size) in enumerate(pieces):
+    sums = [0.0] * PAIR
+    for piece, (start, size) in enumerate(pieces):
         last_copy(piece).wait()
-        more = mix(weights, last_slot, j, start, size)
-        sums = more if start == 0 else sums + more
-        if start + size == rows:
-            seen[me, count - PAIR + j] = sums.astype(seen.dtype)
-            send(LAST_SEEN, count - PAIR + j)
+        sums = [sums[j] + mix(weights, last_slot, j, start, size) for j in range(PAIR)]
+    for j in range(PAIR):
+        seen[me, count - PAIR + j] = sums[j].astype(seen.dtype)
+    send(LAST_SEEN, pl.ds(count - PAIR, PAIR))
 
     received(EARLY_SEEN, pl.ds(0, count - PAIR))
     received(EARLY_STATS, pl.ds(0, steps - 1))
@@ -217,8 +218,7 @@
                 pltpu.VMEM(q.shape, q.dtype),
                 pltpu.VMEM((SLOTS, PAIR, rows, head), k.dtype),
                 pltpu.VMEM((SLOTS, PAIR, rows, head), v.dtype),
-                step_buffers,
-                step_buffers,
+                (step_buffers,) * LEAD,
                 pltpu.VMEM((runs, count, heads, head), q.dtype),
                 pltpu.VMEM((runs, steps, heads, LANES), jnp.float32),
                 pltpu.SemaphoreType.DMA,

time: 48.3 us -> 47.3 us (0.979)
  Pallas kernels: 47.6 us -> 46.6 us
    pallas_call x1, Pallas kernels: 47.6 us -> 46.6 us  [step(): pl.pallas_call(functools.partial(kernel, axis, runs, head ** (-0.5)), out...]
where the time goes in v3:
time: 47.3 us
  Pallas kernels  46.6 us (99%)
  local copies, waits for them, and re-layouts  0.66 us (1%)
    pallas_call x1, Pallas kernels, step(): pl.pallas_call(functools.partial(kernel, axis, runs, head ** (-0.5)), out...  46.6 us

profile of v3, /device:TPU:112, one launch (start us, length us, event | category | flops | bytes accessed | tf_op | source)
XLA Modules:
  0.0 47.3 jit_solution(6481429349571561854)
XLA Ops:
  0.0 46.6 %attend.1 = bf16[32,8,256]{2,1,0:T(8,128)(2,1)S(1)} custom-call(bf16[32,8,256]{2,1,0:T(8,128)(2,1)} %q_hbm.1, bf16[32,4096,256]{2,1,0:T(8,128)(2,1)} %bitcast.k_ref, bf16[32,4096,256]{2,1,0:T(8,128)(2,1)} %bitcast.1.v_ref), custom_call_target="tpu_custom_call" | custom-call | tf_op jit(solution)/shard_map/attend/pallas_call | solution.py:212
  46.6 0.7 %copy.5 = bf16[32,8,256]{2,1,0:T(8,128)(2,1)} copy(bf16[32,8,256]{2,1,0:T(8,128)(2,1)S(1)} %attend.1) | data formatting | bytes 262144
